TPU v7x, 512 devices: a whole 4x8x8 slice. The times are simulated.
512 devices in a mesh: probe: 4 (over x), seq: 128 (over y, z, core).
Axes of the slice: x: 4, y: 8, z: 8, core: 2. Of those that a mesh axis runs over, the one named last changes fastest.
Arguments:
- probe_bits: int32 [4, 128, 16384], P('probe', 'seq'), may hold values from 0 to 1
- noise_var: float32 [128, 16384], P('seq'), may hold values from 0.2 to 12
- kernel_spectrum: float32 [16384, 128], P('seq'), may hold values from 0.05 to 4, as said below
- symbol: float32 [16384, 128], P('seq'), may hold values from 0.3 to 3, as said below
- grad_prev: float32 [16384, 128], P('seq', 'probe'), may hold values from -6 to 6
Outputs:
- residual: float32 [4, 128, 16384], P('probe', 'seq')
- grad_total: float32 [16384, 128], P('seq', 'probe')
Inputs may be any that keep to these rules, and one draw needn't show every extreme that they name: kernel_spectrum at frequency k equals kernel_spectrum at frequency (2097152 - k) mod 2097152. symbol at frequency k equals symbol at frequency (2097152 - k) mod 2097152.
All inputs are finite; a program needn't handle non-finite values.
Results may differ from a plain program's by a relative error of at most 0.00017.
Values sent between devices are 32-bit elements; how exact they have to be, the bound alone decides.
A program may use at most 64 MiB of HBM per device.

v0:
```python
import math
import jax
import jax.numpy as jnp
from jax import lax
from jax.sharding import PartitionSpec as P

highest = lax.Precision.HIGHEST
minor_width = 128


def dft_table(height, breadth, modulus, orient):
    left_index = jnp.arange(height, dtype=jnp.int32)[:, None]
    right_index = jnp.arange(breadth, dtype=jnp.int32)[None, :]
    phases = (
        orient * 2.0 * math.pi / modulus * (left_index * right_index % modulus).astype(jnp.float32)
    )
    return (jnp.cos(phases), jnp.sin(phases))


def complex_product(pattern, real_part, imaginary, cosine_table, sine_table):
    real_cos = jnp.einsum(pattern, real_part, cosine_table, precision=highest)
    real_sin = jnp.einsum(pattern, real_part, sine_table, precision=highest)
    if imaginary is None:
        return (real_cos, real_sin)
    imag_cos = jnp.einsum(pattern, imaginary, cosine_table, precision=highest)
    imag_sin = jnp.einsum(pattern, imaginary, sine_table, precision=highest)
    return (real_cos - imag_sin, real_sin + imag_cos)


def rotate(real_part, imaginary, cosine_table, sine_table):
    return (
        real_part * cosine_table - imaginary * sine_table,
        real_part * sine_table + imaginary * cosine_table,
    )


def forward_rows(series):
    major_len = series.shape[-2]
    length = major_len * minor_width
    cosine_table, sine_table = dft_table(major_len, major_len, major_len, -1.0)
    section_real, section_imag = complex_product(
        "...mi,mk->...ik", series, None, cosine_table, sine_table
    )
    turn_cos, turn_sin = dft_table(minor_width, major_len, length, -1.0)
    twisted_real, twisted_imag = rotate(section_real, section_imag, turn_cos, turn_sin)
    cosine_table, sine_table = dft_table(minor_width, minor_width, minor_width, -1.0)
    return complex_product("...ik,ij->...jk", twisted_real, twisted_imag, cosine_table, sine_table)


def inverse_rows(real_part, imaginary):
    major_len = real_part.shape[-1]
    length = major_len * minor_width
    cosine_table, sine_table = dft_table(minor_width, minor_width, minor_width, 1.0)
    section_real, section_imag = complex_product(
        "...jk,ji->...ik", real_part, imaginary, cosine_table, sine_table
    )
    turn_cos, turn_sin = dft_table(minor_width, major_len, length, 1.0)
    twisted_real, twisted_imag = rotate(section_real, section_imag, turn_cos, turn_sin)
    cosine_table, sine_table = dft_table(major_len, major_len, major_len, 1.0)
    final_real, unused = complex_product(
        "...ik,km->...mi", twisted_real, twisted_imag, cosine_table, sine_table
    )
    return final_real


def global_twiddle(local_rows, major_len, samples, orient):
    row_index = lax.axis_index("seq") * local_rows + jnp.arange(local_rows, dtype=jnp.int32)
    column_index = (
        jnp.arange(minor_width, dtype=jnp.int32)[:, None] * major_len
        + jnp.arange(major_len, dtype=jnp.int32)[None, :]
    )
    phases = (
        orient
        * 2.0
        * math.pi
        / samples
        * (row_index[:, None, None] * column_index[None, :, :] % samples).astype(jnp.float32)
    )
    return (jnp.cos(phases), jnp.sin(phases))


def forward_spectrum(series):
    local_rows = series.shape[1]
    major_len = series.shape[2]
    devices = lax.axis_size("seq")
    all_rows = local_rows * devices
    samples = all_rows * major_len * minor_width
    real_part, imaginary = forward_rows(series)
    turn_cos, turn_sin = global_twiddle(local_rows, major_len, samples, -1.0)
    turned_real, turned_imag = rotate(real_part, imaginary, turn_cos, turn_sin)
    arrived = lax.all_to_all(
        jnp.stack([turned_real, turned_imag]), "seq", split_axis=3, concat_axis=2, tiled=True
    )
    block = minor_width // devices * major_len
    arrived = arrived.reshape(arrived.shape[0], arrived.shape[1], all_rows, block)
    cosine_table, sine_table = dft_table(all_rows, all_rows, all_rows, -1.0)
    return complex_product("zrb,ra->zba", arrived[0], arrived[1], cosine_table, sine_table)


def inverse_field(spectrum_real, spectrum_imag):
    all_rows = spectrum_real.shape[2]
    block = spectrum_real.shape[1]
    devices = lax.axis_size("seq")
    major_len = block * devices // minor_width
    cosine_table, sine_table = dft_table(all_rows, all_rows, all_rows, 1.0)
    back_real, back_imag = complex_product(
        "zba,ar->zrb", spectrum_real, spectrum_imag, cosine_table, sine_table
    )
    stacked = jnp.stack([back_real, back_imag])
    stacked = stacked.reshape(
        stacked.shape[0], stacked.shape[1], all_rows, minor_width // devices, major_len
    )
    arrived = lax.all_to_all(stacked, "seq", split_axis=2, concat_axis=3, tiled=True)
    local_rows = arrived.shape[2]
    samples = all_rows * major_len * minor_width
    turn_cos, turn_sin = global_twiddle(local_rows, major_len, samples, 1.0)
    turned_real, turned_imag = rotate(arrived[0], arrived[1], turn_cos, turn_sin)
    return inverse_rows(turned_real, turned_imag) / samples


def shards(probe_bits, noise_var, kernel_spectrum, symbol, grad_prev):
    field_shape = (
        probe_bits.shape[0],
        probe_bits.shape[1],
        probe_bits.shape[2] // minor_width,
        minor_width,
    )
    sign_field = (2 * probe_bits - 1).astype(jnp.float32).reshape(field_shape)
    noise_field = noise_var.reshape(field_shape[1:])
    samples = kernel_spectrum.shape[1] * noise_var.shape[1]
    base_real, base_imag = forward_spectrum(sign_field)
    scaled_real = base_real / symbol
    scaled_imag = base_imag / symbol
    precond = inverse_field(scaled_real, scaled_imag)
    again_real, again_imag = forward_spectrum(precond)
    circulant = inverse_field(kernel_spectrum * again_real, kernel_spectrum * again_imag)
    kernel_image = circulant + noise_field * precond
    numerator, curvature = lax.psum(
        (jnp.sum(sign_field * precond), jnp.sum(precond * kernel_image)), "seq"
    )
    step_size = numerator / curvature
    residual = sign_field - step_size * kernel_image
    cross_term = lax.psum(jnp.sum(residual * kernel_image), "seq")
    weight = -2.0 * cross_term
    resid_real, resid_imag = forward_spectrum(residual)
    applied = (
        inverse_field(kernel_spectrum * resid_real, kernel_spectrum * resid_imag)
        + noise_field * residual
    )
    adjoint = (
        weight / curvature * sign_field
        - 2.0 * weight * step_size / curvature * kernel_image
        - 2.0 * step_size * applied
    )
    adjoint_real, adjoint_imag = forward_spectrum(adjoint)
    local_grad = -(adjoint_real[0] * base_real[0] + adjoint_imag[0] * base_imag[0]) / (
        samples * symbol * symbol
    )
    probes = lax.axis_size("probe")
    summed = lax.psum(local_grad, "probe")
    share_width = summed.shape[1] // probes
    own_share = lax.dynamic_slice_in_dim(
        summed, lax.axis_index("probe") * share_width, share_width, 1
    )
    grad_total = grad_prev + own_share / probes
    return (residual.reshape(probe_bits.shape), grad_total)


def solution(mesh):
    placed = (
        P("probe", "seq", None),
        P("seq", None),
        P("seq", None),
        P("seq", None),
        P("seq", "probe"),
    )
    return jax.shard_map(
        shards,
        mesh=mesh,
        in_specs=placed,
        out_specs=(P("probe", "seq", None), P("seq", "probe")),
        check_vma=False,
    )
```

profile of v0, /device:TPU:8, one launch (start us, length us, event | category | flops | bytes accessed | tf_op | source)
XLA Modules:
  0.0 741.7 jit_solution(7742233880407343323)
XLA Ops:
  7.2 0.9 add_convert_fusion
  11.2 0.9 subtract_bitcast_fusion.3
  12.2 29.0 %all_to_all.28 = f32[2,1,1,128,128]{4,2,1,0,3:T(1,128)S(1)} all-to-all(f32[2,1,1,128,128]{4,2,1,0,3:T(1,128)S(1)} %copy.13), channel_id=1, replica_groups=mesh['probe'=4,'seq'=128] {'seq'}, dimensions={3} | all-to-all | bytes 262144 | tf_op jit(solution)/shard_map/all_to_all | solution.py:91
  45.9 18.2 %all_to_all.29 = f32[2,1,128,1,128]{4,3,1,0,2:T(1,128)S(1)} all-to-all(f32[2,1,128,1,128]{4,3,1,0,2:T(1,128)S(1)} %copy.14), channel_id=1, replica_groups=mesh['probe'=4,'seq'=128] {'seq'}, dimensions={2} | all-to-all | bytes 262144 | tf_op jit(solution)/shard_map/all_to_all | solution.py:113
  64.1 0.7 fusion.82
  65.6 0.7 convolution_subtract_fusion.13
  66.4 0.7 convolution_add_fusion.10
  67.1 0.8 fusion.43
  67.9 0.8 fusion.16
  71.7 0.9 subtract_bitcast_fusion.2
  72.8 18.1 %all_to_all.30 = f32[2,1,1,128,128]{4,2,1,0,3:T(1,128)S(1)} all-to-all(f32[2,1,1,128,128]{4,2,1,0,3:T(1,128)S(1)} %copy.17), channel_id=1, replica_groups=mesh['probe'=4,'seq'=128] {'seq'}, dimensions={3} | all-to-all | bytes 262144 | tf_op jit(solution)/shard_map/all_to_all | solution.py:91
  95.5 17.8 %all_to_all.31 = f32[2,1,128,1,128]{4,3,1,0,2:T(1,128)S(1)} all-to-all(f32[2,1,128,1,128]{4,3,1,0,2:T(1,128)S(1)} %copy.18), channel_id=1, replica_groups=mesh['probe'=4,'seq'=128] {'seq'}, dimensions={2} | all-to-all | bytes 262144 | tf_op jit(solution)/shard_map/all_to_all | solution.py:113
  113.4 0.7 fusion.80
  114.9 0.7 convolution_subtract_fusion.8
  115.6 0.7 convolution_add_fusion.6
  116.4 0.8 fusion.36
  117.2 1.4 multiply_reduce_fusion.1
  118.6 213.3 %all-reduce = (f32[]{:T(128)}, f32[]{:T(128)}) all-reduce(f32[]{:T(128)} %get-tuple-element.7, f32[]{:T(128)} %get-tuple-element.6), channel_id=1, replica_groups=mesh['probe'=4,'seq'=128] {'seq'}, use_global_device_ids=true, to_apply=%region_1.2 | all-reduce | flops 2 | bytes 16 | tf_op jit(solution)/shard_map/psum | solution.py:138
  337.0 0.9 subtract_bitcast_fusion.1
  338.0 53.9 %all_to_all.32 = f32[2,1,1,128,128]{4,2,1,0,3:T(1,128)S(1)} all-to-all(f32[2,1,1,128,128]{4,2,1,0,3:T(1,128)S(1)} %copy.21), channel_id=1, replica_groups=mesh['probe'=4,'seq'=128] {'seq'}, dimensions={3} | all-to-all | bytes 262144 | tf_op jit(solution)/shard_map/all_to_all | solution.py:91
  396.0 0.8 copy.22
  396.8 6.6 all-to-all-start.5
  403.4 217.7 %psum.30 = f32[]{:T(128)} all-reduce(f32[]{:T(128)} %get-tuple-element.10), channel_id=1, replica_groups=mesh['probe'=4,'seq'=128] {'seq'}, use_global_device_ids=true, to_apply=%region_5.6 | all-reduce | flops 1 | bytes 8 | tf_op jit(solution)/shard_map/psum | solution.py:143
  625.4 0.7 convolution_subtract_fusion.3
  626.2 0.7 convolution_add_fusion.2
  626.9 0.8 fusion.29
  627.7 0.8 fusion.20
  631.5 0.9 subtract_bitcast_fusion
  632.6 53.0 %all_to_all.33 = f32[2,1,1,128,128]{4,2,1,0,3:T(1,128)S(1)} all-to-all(f32[2,1,1,128,128]{4,2,1,0,3:T(1,128)S(1)} %copy.25), channel_id=1, replica_groups=mesh['probe'=4,'seq'=128] {'seq'}, dimensions={3} | all-to-all | bytes 262144 | tf_op jit(solution)/shard_map/all_to_all | solution.py:91
  687.1 1.1 fusion.21
  689.0 44.0 %all-reduce.3.cloned.1.call-done = f32[128,128]{1,0:T(8,128)} async-done(((f32[128,128]{1,0:T(8,128)}), f32[128,128]{1,0:T(8,128)}) %all-reduce.3.cloned.1.call-update) | async-done | bytes 65552 | tf_op jit(solution)/shard_map/psum | solution.py:160
  733.0 0.9 multiply_add_fusion
  (88 shorter events, 32.7 us)
Async XLA Ops:
  42.3 0.8 copy-start.4
  91.4 0.8 copy-start.2
  116.4 0.8 copy-start.3
  333.9 293.8 %copy-start = (f32[128,128]{1,0:T(8,128)}, f32[128,128]{1,0:T(8,128)S(1)}, u32[]{:S(2)}) copy-start(f32[128,128]{1,0:T(8,128)S(1)} %get-tuple-element.11) | copy-start | bytes 196612
  396.8 227.0 %all-to-all-start.5 = ((f32[2,1,128,1,128]{4,3,1,0,2:T(1,128)}), f32[2,1,128,1,128]{4,3,1,0,2:T(1,128)S(1)}, u32[]{:S(2)}, u32[]{:S(2)}) async-start(f32[2,1,128,1,128]{4,3,1,0,2:T(1,128)} %copy.22), calls=%async_computation.5 | async-start | bytes 262144 | tf_op jit(solution)/shard_map/all_to_all | solution.py:113
  403.4 329.7 %all-reduce.3.cloned.1.call-start = ((), (), s32[]{:S(2)}) async-start(), calls=%async_computation.7 | async-start | bytes 131072 | tf_op jit(solution)/shard_map/psum | solution.py:160
  688.2 0.7 copy-start.1
Sparse Core Ops, SparseCore 0:
  688.3 44.6 all-reduce.2
where the time goes:
time: 750 us; the launch traced here: 742 us
  blocking collectives  621 us (83%)
  waiting for transfers between devices  44.1 us (6%)
  matrix products  43.9 us (6%)
  between operations  18.9 us (3%)
    psum x1, blocking collectives, shards(): cross_term = lax.psum(jnp.sum(residual * kernel_image), 'seq')  218 us
    psum x1, blocking collectives, shards(): lax.psum((jnp.sum(sign_field * precond), jnp.sum(precond * kernel_image))...  213 us
    all_to_all x4, blocking collectives, forward_spectrum(): lax.all_to_all(jnp.stack([turned_real, turned_imag]), 'seq', split_axis=3...  154 us
    psum x1, waiting for transfers between devices, shards(): summed = lax.psum(local_grad, 'probe')  44 us
    all_to_all x2, blocking collectives, inverse_field(): lax.all_to_all(stacked, 'seq', split_axis=2, concat_axis=3, tiled=True)  36 us
  transfers between devices with their start and end apart: 2, of which 1 were waited for; matrix products, arithmetic and copies ran while one was open for 0% of the time, Pallas kernels for 0%

commit v1 on v0

--- a/solution.py
+++ b/solution.py
@@ -157,7 +157,7 @@
         samples * symbol * symbol
     )
     probes = lax.axis_size("probe")
-    summed = lax.psum(local_grad, "probe")
+    summed = jnp.sum(lax.all_gather(local_grad, "probe"), axis=0)
     share_width = summed.shape[1] // probes
     own_share = lax.dynamic_slice_in_dim(
         summed, lax.axis_index("probe") * share_width, share_width, 1

time: 750 us -> 705 us (0.940)
  the two profiles are of different devices: /device:TPU:8 before, /device:TPU:2 now
where the time goes in v1:
time: 705 us; the launch traced here: 696 us
  blocking collectives  616 us (87%)
  matrix products  43.2 us (6%)
  starting transfers between devices  12.6 us (2%)
  waiting for transfers between devices  12.2 us (2%)
    psum x1, blocking collectives, shards(): cross_term = lax.psum(jnp.sum(residual * kernel_image), 'seq')  253 us
    psum x1, blocking collectives, shards(): lax.psum((jnp.sum(sign_field * precond), jnp.sum(precond * kernel_image))...  248 us
    all_to_all x3, blocking collectives, forward_spectrum(): lax.all_to_all(jnp.stack([turned_real, turned_imag]), 'seq', split_axis=3...  67.4 us
    all_to_all x2, blocking collectives, inverse_field(): lax.all_to_all(stacked, 'seq', split_axis=2, concat_axis=3, tiled=True)  35.9 us
  transfers between devices with their start and end apart: 2, of which 1 were waited for; matrix products, arithmetic and copies ran while one was open for 0% of the time, Pallas kernels for 0%

profile of v1, /device:TPU:2, one launch (start us, length us, event | category | flops | bytes accessed | tf_op | source)
XLA Modules:
  0.0 696.3 jit_solution(2999850474396409225)
XLA Ops:
  0.6 0.9 add_convert_fusion
  4.6 0.9 subtract_bitcast_fusion.3
  5.7 29.9 %all_to_all.28 = f32[2,1,1,128,128]{4,2,1,0,3:T(1,128)S(1)} all-to-all(f32[2,1,1,128,128]{4,2,1,0,3:T(1,128)S(1)} %copy.7), channel_id=1, replica_groups=mesh['probe'=4,'seq'=128] {'seq'}, dimensions={3} | all-to-all | bytes 262144 | tf_op jit(solution)/shard_map/all_to_all | solution.py:91
  40.2 18.1 %all_to_all.29 = f32[2,1,128,1,128]{4,3,1,0,2:T(1,128)S(1)} all-to-all(f32[2,1,128,1,128]{4,3,1,0,2:T(1,128)S(1)} %copy.8), channel_id=1, replica_groups=mesh['probe'=4,'seq'=128] {'seq'}, dimensions={2} | all-to-all | bytes 262144 | tf_op jit(solution)/shard_map/all_to_all | solution.py:113
  58.4 0.7 fusion.82
  59.1 0.7 fusion.88
  59.9 0.7 convolution_subtract_fusion.13
  60.6 0.7 convolution_add_fusion.10
  61.4 0.8 fusion.43
  62.1 0.8 fusion.16
  66.0 0.9 subtract_bitcast_fusion.2
  67.0 18.1 %all_to_all.30 = f32[2,1,1,128,128]{4,2,1,0,3:T(1,128)S(1)} all-to-all(f32[2,1,1,128,128]{4,2,1,0,3:T(1,128)S(1)} %copy.11), channel_id=1, replica_groups=mesh['probe'=4,'seq'=128] {'seq'}, dimensions={3} | all-to-all | bytes 262144 | tf_op jit(solution)/shard_map/all_to_all | solution.py:91
  89.7 17.8 %all_to_all.31 = f32[2,1,128,1,128]{4,3,1,0,2:T(1,128)S(1)} all-to-all(f32[2,1,128,1,128]{4,3,1,0,2:T(1,128)S(1)} %copy.12), channel_id=1, replica_groups=mesh['probe'=4,'seq'=128] {'seq'}, dimensions={2} | all-to-all | bytes 262144 | tf_op jit(solution)/shard_map/all_to_all | solution.py:113
  107.7 0.7 fusion.80
  108.4 0.7 fusion.86
  109.2 0.7 convolution_subtract_fusion.8
  109.9 0.7 convolution_add_fusion.6
  110.7 0.8 fusion.36
  111.5 1.4 multiply_reduce_fusion.1
  112.9 248.0 %all-reduce = (f32[]{:T(128)}, f32[]{:T(128)}) all-reduce(f32[]{:T(128)} %get-tuple-element.5, f32[]{:T(128)} %get-tuple-element.4), channel_id=1, replica_groups=mesh['probe'=4,'seq'=128] {'seq'}, use_global_device_ids=true, to_apply=%region_1.2 | all-reduce | flops 2 | bytes 16 | tf_op jit(solution)/shard_map/psum | solution.py:138
  365.9 0.9 subtract_bitcast_fusion.1
  366.9 19.3 %all_to_all.32 = f32[2,1,1,128,128]{4,2,1,0,3:T(1,128)S(1)} all-to-all(f32[2,1,1,128,128]{4,2,1,0,3:T(1,128)S(1)} %copy.15), channel_id=1, replica_groups=mesh['probe'=4,'seq'=128] {'seq'}, dimensions={3} | all-to-all | bytes 262144 | tf_op jit(solution)/shard_map/all_to_all | solution.py:91
  390.3 0.8 copy.16
  391.1 6.2 all-to-all-start.5
  397.2 252.7 %psum.23 = f32[]{:T(128)} all-reduce(f32[]{:T(128)} %get-tuple-element.8), channel_id=1, replica_groups=mesh['probe'=4,'seq'=128] {'seq'}, use_global_device_ids=true, to_apply=%region_5.6 | all-reduce | flops 1 | bytes 8 | tf_op jit(solution)/shard_map/psum | solution.py:143
  655.7 0.8 fusion.29
  656.5 0.8 fusion.20
  660.3 0.9 subtract_bitcast_fusion
  661.2 0.8 copy.19
  662.0 6.5 all-to-all-start.6
  668.6 12.2 %all-to-all-done.6 = f32[2,1,1,128,128]{4,2,1,0,3:T(1,128)S(1)} async-done(((f32[2,1,1,128,128]{4,2,1,0,3:T(1,128)}), f32[2,1,1,128,128]{4,2,1,0,3:T(1,128)S(1)}, u32[]{:S(2)}, u32[]{:S(2)}) %all-to-all-start.6) | async-done | bytes 131104 | tf_op jit(solution)/shard_map/all_to_all | solution.py:91
  682.8 12.5 %all-gather = f32[512,128]{1,0:T(8,128)S(1)} all-gather(f32[128,128]{1,0:T(8,128)S(1)} %fusion.21), channel_id=2, replica_groups=mesh['probe'=4,'seq'=128] {'probe'}, dimensions={0}, use_global_device_ids=true | all-gather | bytes 327680 | tf_op jit(solution)/shard_map/all_gather | solution.py:160
  (88 shorter events, 32.4 us)
Async XLA Ops:
  36.6 0.8 copy-start.4
  85.7 0.8 copy-start.2
  110.7 0.8 copy-start.3
  362.8 293.7 %copy-start = (f32[128,128]{1,0:T(8,128)}, f32[128,128]{1,0:T(8,128)S(1)}, u32[]{:S(2)}) copy-start(f32[128,128]{1,0:T(8,128)S(1)} %get-tuple-element.9) | copy-start | bytes 196612
  391.1 261.5 %all-to-all-start.5 = ((f32[2,1,128,1,128]{4,3,1,0,2:T(1,128)}), f32[2,1,128,1,128]{4,3,1,0,2:T(1,128)S(1)}, u32[]{:S(2)}, u32[]{:S(2)}) async-start(f32[2,1,128,1,128]{4,3,1,0,2:T(1,128)} %copy.16), calls=%async_computation.5 | async-start | bytes 262144 | tf_op jit(solution)/shard_map/all_to_all | solution.py:113
  662.0 6.5 copy-start.1
  662.0 18.8 %all-to-all-start.6 = ((f32[2,1,1,128,128]{4,2,1,0,3:T(1,128)}), f32[2,1,1,128,128]{4,2,1,0,3:T(1,128)S(1)}, u32[]{:S(2)}, u32[]{:S(2)}) async-start(f32[2,1,1,128,128]{4,2,1,0,3:T(1,128)} %copy.19), calls=%async_computation.6 | async-start | bytes 262144 | tf_op jit(solution)/shard_map/all_to_all | solution.py:91
